TPU v7x, 128 devices: a whole 4x4x4 slice. The times are simulated.
128 devices in a mesh: clip: 4 (over y_hi, core), frame: 32 (over z, x, y_lo).
Axes of the slice: x: 4, y: 4 (y_hi: 2, y_lo: 2; y = y_hi * 2 + y_lo), z: 4, core: 2. Of those that a mesh axis runs over, the one named last changes fastest.
Arguments:
- video: bfloat16 [512, 512, 512], P(('clip', 'frame')), parts along dimension 0, may hold values from -6 to 6
- timestep: int32 [4], P('clip'), parts along dimension 0, may hold values from 0 to 999
- cond_weight: bfloat16 [128, 2048], replicated, may hold values from -0.5 to 0.5
- spatial_gain: float32 [512], replicated, may hold values from 0.25 to 1.75
- spatial_qkv: bfloat16 [512, 1536], replicated, may hold values from -0.25 to 0.25
- spatial_out: bfloat16 [512, 512], replicated, may hold values from -0.25 to 0.25
- temporal_gain: float32 [512], replicated, may hold values from 0.25 to 1.75
- temporal_qkv: bfloat16 [512, 1536], replicated, may hold values from -0.25 to 0.25
- temporal_out: bfloat16 [512, 512], replicated, may hold values from -0.25 to 0.25
- merge_weight: bfloat16 [4096, 1024], replicated, may hold values from -0.09375 to 0.09375
- coarse_gain: float32 [1024], replicated, may hold values from 0.25 to 1.75
- coarse_qkv: bfloat16 [1024, 3072], replicated, may hold values from -0.1875 to 0.1875
- coarse_out: bfloat16 [1024, 1024], replicated, may hold values from -0.1875 to 0.1875
- up_weight: bfloat16 [1024, 512], replicated, may hold values from -0.1875 to 0.1875
Outputs:
- denoised: bfloat16 [512, 512, 512], P(('clip', 'frame')), parts along dimension 0
There are 4 independent parts, one for each index of `clip`. A program takes and returns all parts, laid end to end along the dimension named above; an argument that names none is the same for every part. Nothing has to cross between parts.
All inputs are finite; a program needn't handle non-finite values.
Results may differ from a plain program's by a relative error of at most 0.015.
Values may be sent and summed in bfloat16 or wider, within the bound.
A program may use at most 192 MiB of HBM per device.

v0:
```python
import math

import jax
import jax.numpy as jnp
from jax import lax
from jax.experimental import pallas as pl
from jax.experimental.pallas import tpu as pltpu
from jax.sharding import PartitionSpec as P

D = 512
DC = 1024
HEAD = 64
FREQ = 64
GROUP = 32
MESH = pl.DeviceIdType.MESH
F32 = jnp.float32
BF16 = jnp.bfloat16
QSCALE = math.log2(math.e) / math.sqrt(HEAD)

OFFSETS = sorted(
    [(a, b, d) for a in range(4) for b in range(4) for d in range(2) if (a, b, d) != (0, 0, 0)],
    key=lambda o: -(min(o[0], 4 - o[0]) + min(o[1], 4 - o[1]) + o[2]),
)


def dot(a, b):
    return jnp.dot(a, b, preferred_element_type=F32)


def dot_t(a, b):
    return lax.dot_general(a, b, (((1,), (1,)), ((), ())), preferred_element_type=F32)


def onehot(rows, columns, column_of):
    r = lax.broadcasted_iota(jnp.int32, (rows, columns), 0)
    c = lax.broadcasted_iota(jnp.int32, (rows, columns), 1)
    return jnp.where(c == column_of(r), 1.0, 0.0).astype(BF16)


def rms(x):
    return x * lax.rsqrt(jnp.mean(x * x, axis=-1, keepdims=True) + 1e-06)


def pair_attention(q2, kst, vst, ones, keys):
    s = dot_t(q2, kst)
    s_lo, s_hi = s[:, :keys], s[:, keys:]
    p_lo = jnp.exp2(s_lo - jnp.max(s_lo, axis=-1, keepdims=True)).astype(BF16)
    p_hi = jnp.exp2(s_hi - jnp.max(s_hi, axis=-1, keepdims=True)).astype(BF16)
    p = jnp.concatenate([p_lo, p_hi], axis=1)
    o = dot(p, jnp.concatenate([vst, ones], axis=1))
    return (o[:, :128] / o[:, 128:]).astype(BF16)


def kernel(
    video, emb, cond, sgain, sqkv, sout, tgain, tqkv, tout, merge, cgain, cqkv, cout, up,
    out,
    vid, wcond, wsq, wso, wtq, wto, wm, wcq, wco, wup,
    sq, skst, svst, ones_s, smix,
    sbuf1, recv1,
    perm, xt, tq, tkst, tvst, ones_t, tmix,
    sbuf2, cbuf, recv2,
    c0, cq, ck, cv, cmix, zs, zr,
    modv, lsem, vsem, osem, ss1, rs1, ss2, rs2, ss3, rs3,
):
    clip = lax.axis_index("clip")
    me = lax.axis_index("frame")
    z, x, y = me // 8, lax.rem(me // 2, 4), lax.rem(me, 2)

    def peer(o):
        return lax.rem(z + o[0], 4) * 8 + lax.rem(x + o[1], 4) * 2 + lax.rem(y + o[2], 2)

    barrier = pltpu.get_barrier_semaphore()
    for o in OFFSETS:
        pl.semaphore_signal(barrier, inc=1, device_id=(clip, peer(o)), device_id_type=MESH)

    weights = [
        (cond, wcond), (sqkv, wsq), (sout, wso), (tqkv, wtq), (tout, wto),
        (merge, wm), (cqkv, wcq), (cout, wco), (up, wup),
    ]
    wcopy = [pltpu.make_async_copy(a, b, lsem.at[i]) for i, (a, b) in enumerate(weights)]
    vcopy = [pltpu.make_async_copy(video.at[f], vid.at[f], vsem.at[f]) for f in range(4)]
    vcopy[0].start()
    for i in range(3):
        wcopy[i].start()
    for f in range(1, 4):
        vcopy[f].start()

    lane = lax.broadcasted_iota(jnp.int32, (1, 128), 1)
    lo = jnp.where(lane < HEAD, 1.0, 0.0).astype(F32)
    hi = 1.0 - lo
    ones_s[0:512, :] = jnp.broadcast_to(lo, (512, 128)).astype(BF16)
    ones_s[512:1024, :] = jnp.broadcast_to(hi, (512, 128)).astype(BF16)
    ones_t[0:128, :] = jnp.broadcast_to(lo, (128, 128)).astype(BF16)
    ones_t[128:256, :] = jnp.broadcast_to(hi, (128, 128)).astype(BF16)
    perm[0] = onehot(256, 256, lambda r: (r & 15) * 16 + (r >> 4))
    perm[1] = onehot(
        256, 256,
        lambda r: ((r & 3) * 4 + ((r >> 5) & 3)) * 16 + ((r >> 2) & 7) * 2 + (r >> 7),
    )
    perm[2] = onehot(256, 256, lambda r: (r & 63) * 4 + (r >> 6))

    wcopy[0].wait()
    modv[...] = jnp.sum(emb[...] * wcond[...].astype(F32), axis=0, keepdims=True)
    sg = sgain[...] * (1.0 + modv[:, 0:D])
    shs = modv[:, D : 2 * D]
    tg = tgain[...] * (1.0 + modv[:, 2 * D : 3 * D])
    sht = modv[:, 3 * D : 4 * D]

    wcopy[1].wait()
    wcopy[2].wait()
    for f in range(4):
        vcopy[f].wait()
    for i in range(3, 9):
        wcopy[i].start()
    pl.semaphore_wait(barrier, len(OFFSETS))

    def frame_step(f, carry):
        xf = vid[f].astype(F32)
        normed = (rms(xf) * sg + shs).astype(BF16)
        sq[...] = (dot(normed, wsq[:, 0:D]) * QSCALE).astype(BF16)
        for p in range(4):
            k2 = dot(normed, wsq[:, D + p * 128 : D + (p + 1) * 128])
            skst[p, 0:512] = (k2 * lo).astype(BF16)
            skst[p, 512:1024] = (k2 * hi).astype(BF16)
            v2 = dot(normed, wsq[:, 2 * D + p * 128 : 2 * D + (p + 1) * 128])
            svst[p, 0:512] = (v2 * lo).astype(BF16)
            svst[p, 512:1024] = (v2 * hi).astype(BF16)

        for p in range(4):
            def rows_step(i, c, p=p):
                rows = pl.ds(pl.multiple_of(i * 256, 256), 256)
                smix[rows, p * 128 : (p + 1) * 128] = pair_attention(
                    sq[rows, p * 128 : (p + 1) * 128], skst[p], svst[p], ones_s[...], 512
                )
                return c

            lax.fori_loop(0, 2, rows_step, 0)
        fine1 = (vid[f].astype(F32) + dot(smix[...], wso[...])).astype(BF16)
        sbuf1[f] = fine1
        own = pl.ds(pl.multiple_of(me * 16, 16), 16)
        recv1[me * 4 + f] = sbuf1[f, own, :]
        for o in OFFSETS:
            to = peer(o)
            pltpu.make_async_remote_copy(
                src_ref=sbuf1.at[f, pl.ds(pl.multiple_of(to * 16, 16), 16), :],
                dst_ref=recv1.at[me * 4 + f],
                send_sem=ss1,
                recv_sem=rs1,
                device_id=(clip, to),
                device_id_type=MESH,
            ).start()
        return carry

    lax.fori_loop(0, 4, frame_step, 0)

    wcopy[3].wait()
    wcopy[4].wait()
    pltpu.make_async_copy(recv1.at[pl.ds(0, 124)], recv1.at[pl.ds(0, 124)], rs1).wait()

    def group_step(g, carry):
        frames = pl.ds(pl.multiple_of(g * 16, 16), 16)
        xg = recv1[frames].reshape(256, D)
        yg = dot(perm[0], xg)
        xt[:, frames, :] = yg.astype(BF16).reshape(16, 16, D)
        normed = (rms(yg) * tg + sht).astype(BF16)
        tq[:, frames, :] = (dot(normed, wtq[:, 0:D]) * QSCALE).astype(BF16).reshape(16, 16, D)
        high = pl.ds(pl.multiple_of(128 + g * 16, 16), 16)
        for p in range(4):
            k2 = dot(normed, wtq[:, D + p * 128 : D + (p + 1) * 128])
            tkst[:, p, frames, :] = (k2 * lo).astype(BF16).reshape(16, 16, 128)
            tkst[:, p, high, :] = (k2 * hi).astype(BF16).reshape(16, 16, 128)
            v2 = dot(normed, wtq[:, 2 * D + p * 128 : 2 * D + (p + 1) * 128])
            tvst[:, p, frames, :] = (v2 * lo).astype(BF16).reshape(16, 16, 128)
            tvst[:, p, high, :] = (v2 * hi).astype(BF16).reshape(16, 16, 128)
        return carry

    lax.fori_loop(0, 8, group_step, 0)

    def token_step(t, carry):
        for p in range(4):
            tmix[t, :, p * 128 : (p + 1) * 128] = pair_attention(
                tq[t, :, p * 128 : (p + 1) * 128], tkst[t, p], tvst[t, p], ones_t[...], 128
            )
        tmix[t] = (xt[t].astype(F32) + dot(tmix[t], wto[...])).astype(BF16)
        return carry

    lax.fori_loop(0, 16, token_step, 0)

    def back_step(g, carry):
        frames = pl.ds(pl.multiple_of(g * 16, 16), 16)
        fg = tmix[:, frames, :].reshape(256, D)
        sbuf2[frames] = dot(perm[0], fg).astype(BF16).reshape(16, 16, D)
        slabs = dot(perm[1], fg).astype(BF16)
        rows = pl.ds(pl.multiple_of(g * 32, 32), 32)
        for s in range(8):
            cbuf[rows, s * D : (s + 1) * D] = slabs[s * 32 : (s + 1) * 32, :]
        return carry

    lax.fori_loop(0, 8, back_step, 0)

    mine = pl.ds(pl.multiple_of(me * 16, 16), 16)
    recv2[:, mine, :] = sbuf2[pl.ds(me * 4, 4)]
    for o in OFFSETS:
        to = peer(o)
        pltpu.make_async_remote_copy(
            src_ref=sbuf2.at[pl.ds(to * 4, 4)],
            dst_ref=recv2.at[:, mine, :],
            send_sem=ss2,
            recv_sem=rs2,
            device_id=(clip, to),
            device_id_type=MESH,
        ).start()

    for i in range(5, 9):
        wcopy[i].wait()
    c0[...] = dot(perm[2], dot(cbuf[...], wm[...]).astype(BF16)).astype(BF16)
    normed = (rms(c0[...].astype(F32)) * cgain[...]).astype(BF16)
    cq[...] = (dot(normed, wcq[:, 0:DC]) * QSCALE).astype(BF16)
    ck[...] = dot(normed, wcq[:, DC : 2 * DC]).astype(BF16)
    cv[...] = dot(normed, wcq[:, 2 * DC : 3 * DC]).astype(BF16)
    lane4 = lax.broadcasted_iota(jnp.int32, (64, 256), 1) >> 6
    block4 = jnp.concatenate(
        [jnp.where(lane4 == h, 1.0, 0.0).astype(BF16) for h in range(4)], axis=0
    )
    low = lax.broadcasted_iota(jnp.int32, (64, 128), 1) < HEAD

    def cell_step(b, carry):
        rows = pl.ds(pl.multiple_of(b * 64, 64), 64)
        for hg in range(4):
            lanes = slice(hg * 256, (hg + 1) * 256)
            k4, v4 = ck[rows, lanes], cv[rows, lanes]
            s = dot_t(cq[rows, lanes], jnp.concatenate([k4] * 4, axis=0) * block4)
            parts = []
            for half in range(2):
                sh = s[:, half * 128 : (half + 1) * 128]
                m_lo = jnp.max(jnp.where(low, sh, -jnp.inf), axis=-1, keepdims=True)
                m_hi = jnp.max(jnp.where(low, -jnp.inf, sh), axis=-1, keepdims=True)
                parts.append(jnp.exp2(sh - jnp.where(low, m_lo, m_hi)).astype(BF16))
            p = jnp.concatenate(parts, axis=1)
            o = dot(p, jnp.concatenate([v4] * 4, axis=0) * block4)
            cmix[rows, lanes] = (o / dot(p, block4)).astype(BF16)
        return carry

    lax.fori_loop(0, 4, cell_step, 0)
    coarse1 = (c0[...].astype(F32) + dot(cmix[...], wco[...])).astype(BF16)
    upped = dot(coarse1, wup[...]).astype(BF16)

    def pick(half):
        r = lax.broadcasted_iota(jnp.int32, (512, 256), 0)
        c = lax.broadcasted_iota(jnp.int32, (512, 256), 1)
        hit = (c == (r & 3) * 64 + (r >> 4) * 2 + ((r >> 2) & 1)) & (((r >> 3) & 1) == half)
        return jnp.where(hit, 1.0, 0.0).astype(BF16)

    zs[...] = (dot(pick(0), upped[:, :256]) + dot(pick(1), upped[:, 256:])).astype(BF16)
    zr[mine, :] = zs[mine, :]
    for o in OFFSETS:
        to = peer(o)
        pltpu.make_async_remote_copy(
            src_ref=zs.at[pl.ds(pl.multiple_of(to * 16, 16), 16), :],
            dst_ref=zr.at[mine, :],
            send_sem=ss3,
            recv_sem=rs3,
            device_id=(clip, to),
            device_id_type=MESH,
        ).start()

    pltpu.make_async_copy(
        recv2.at[:, pl.ds(0, 496), :], recv2.at[:, pl.ds(0, 496), :], rs2
    ).wait()
    pltpu.make_async_copy(zr.at[pl.ds(0, 496)], zr.at[pl.ds(0, 496)], rs3).wait()
    ocopy = []
    for j in range(2):
        for half in range(2):
            spread = onehot(256, 256, lambda r: (r & 240) + half * 8 + j * 4 + ((r >> 2) & 3))
            for k in range(2):
                rows = slice(k * 256, (k + 1) * 256)
                lanes = slice(half * 256, (half + 1) * 256)
                u = dot(spread, zr[rows, :])
                for f in (2 * j, 2 * j + 1):
                    vid[f, rows, lanes] = (recv2[f, rows, lanes].astype(F32) + u).astype(BF16)
        for f in (2 * j, 2 * j + 1):
            cp = pltpu.make_async_copy(vid.at[f], out.at[f], osem.at[f])
            cp.start()
            ocopy.append(cp)
    pltpu.make_async_copy(sbuf1.at[:, pl.ds(0, 496), :], sbuf1.at[:, pl.ds(0, 496), :], ss1).wait()
    pltpu.make_async_copy(sbuf2.at[pl.ds(0, 124)], sbuf2.at[pl.ds(0, 124)], ss2).wait()
    pltpu.make_async_copy(zs.at[pl.ds(0, 496)], zs.at[pl.ds(0, 496)], ss3).wait()
    for cp in ocopy:
        cp.wait()


def body(
    video, timestep, cond_weight, spatial_gain, spatial_qkv, spatial_out, temporal_gain,
    temporal_qkv, temporal_out, merge_weight, coarse_gain, coarse_qkv, coarse_out, up_weight,
):
    counter = jnp.arange(FREQ, dtype=F32)
    frequency = jnp.exp(counter * (-math.log(10000.0) / FREQ))
    angles = timestep.astype(F32)[0] * frequency
    emb = jnp.concatenate([jnp.sin(angles), jnp.cos(angles)])[:, None]
    any_, vm = pl.BlockSpec(memory_space=pl.ANY), pl.BlockSpec(memory_space=pltpu.VMEM)
    b = lambda *shape: pltpu.VMEM(shape, BF16)
    return pl.pallas_call(
        kernel,
        name="denoise",
        out_shape=jax.ShapeDtypeStruct(video.shape, BF16),
        in_specs=[any_, vm, any_, vm, any_, any_, vm, any_, any_, any_, vm, any_, any_, any_],
        out_specs=any_,
        scratch_shapes=[
            b(4, 512, D), b(128, 2048), b(D, 3 * D), b(D, D), b(D, 3 * D), b(D, D),
            b(8 * D, DC), b(DC, 3 * DC), b(DC, DC), b(DC, D),
            b(512, D), b(4, 1024, 128), b(4, 1024, 128), b(1024, 128), b(512, D),
            b(4, 512, D), b(128, 16, D),
            b(3, 256, 256), b(16, 128, D), b(16, 128, D), b(16, 4, 256, 128),
            b(16, 4, 256, 128), b(256, 128), b(16, 128, D),
            b(128, 16, D), b(256, 8 * D), b(4, 512, D),
            b(256, DC), b(256, DC), b(256, DC), b(256, DC), b(256, DC), b(512, 256), b(512, 256),
            pltpu.VMEM((1, 4 * D), F32),
            pltpu.SemaphoreType.DMA((9,)), pltpu.SemaphoreType.DMA((4,)),
            pltpu.SemaphoreType.DMA((4,)),
        ] + [pltpu.SemaphoreType.DMA] * 6,
        compiler_params=pltpu.CompilerParams(
            collective_id=0, has_side_effects=True, vmem_limit_bytes=67_000_000
        ),
    )(
        video, emb, cond_weight, spatial_gain[None], spatial_qkv, spatial_out,
        temporal_gain[None], temporal_qkv, temporal_out, merge_weight, coarse_gain[None],
        coarse_qkv, coarse_out, up_weight,
    )


def solution(mesh):
    return jax.shard_map(
        body,
        mesh=mesh,
        in_specs=(P(("clip", "frame"), None, None), P("clip")) + (P(),) * 12,
        out_specs=P(("clip", "frame"), None, None),
        check_vma=False,
    )
```

profile of v0, /device:TPU:2, one launch (start us, length us, event | category | flops | bytes accessed | tf_op | source)
XLA Modules:
  0.0 106.8 jit_solution(7043172296229450189)
XLA Ops:
  0.7 0.1 maximum_bitcast_fusion
  0.8 0.8 copy.15.emb
  1.5 102.2 %denoise.1 = bf16[4,512,512]{2,1,0:T(8,128)(2,1)} custom-call(bf16[4,512,512]{2,1,0:T(8,128)(2,1)} %video.1, f32[128,1]{1,0:T(8,128)} %copy.15.emb, bf16[128,2048]{1,0:T(8,128)(2,1)} %cond.1, f32[1,512]{1,0:T(1,128)} %bitcast.7, bf16[512,1536]{1,0:T(8,128)(2,1)} %sqkv.1, bf16[512,512]{1,0:T(8,128)(2,1)} %sout.1, f32[1,512]{1,0:T(1,128)} %bitcast.8, ...), custom_call_target="tpu_custom_call" | custom-call | tf_op jit(solution)/shard_map/denoise/pallas_call | solution.py:302
  103.8 3.0 %copy.18 = bf16[4,512,512]{2,1,0:T(8,128)(2,1)} copy(bf16[4,512,512]{2,1,0:T(8,128)(2,1)} %denoise.1) | data formatting | bytes 4194304
  (1 shorter events, 0.0 us)
where the time goes:
time: 107 us
  Pallas kernels  102 us (95%)
  local copies, waits for them, and re-layouts  3.8 us (4%)
    pallas_call x1, Pallas kernels, body(): pl.pallas_call(kernel, name='denoise', out_shape=jax.ShapeDtypeStruct(vid...  102 us
    unnamed x1, local copies, waits for them, and re-layouts  3.05 us

commit v1 on v0

v1 whole, which is shorter than its diff:
```python
import math

import jax
import jax.numpy as jnp
from jax import lax
from jax.experimental import pallas as pl
from jax.experimental.pallas import tpu as pltpu
from jax.sharding import PartitionSpec as P

D = 512
DC = 1024
HEAD = 64
FREQ = 64
GROUP = 32
MESH = pl.DeviceIdType.MESH
F32 = jnp.float32
BF16 = jnp.bfloat16
QSCALE = math.log2(math.e) / math.sqrt(HEAD)

OFFSETS = sorted(
    [(a, b, d) for a in range(4) for b in range(4) for d in range(2) if (a, b, d) != (0, 0, 0)],
    key=lambda o: -(min(o[0], 4 - o[0]) + min(o[1], 4 - o[1]) + o[2]),
)


def dot(a, b):
    return jnp.dot(a, b, preferred_element_type=F32)


def dot_t(a, b):
    return lax.dot_general(a, b, (((1,), (1,)), ((), ())), preferred_element_type=F32)


def onehot(rows, columns, column_of):
    r = lax.broadcasted_iota(jnp.int32, (rows, columns), 0)
    c = lax.broadcasted_iota(jnp.int32, (rows, columns), 1)
    return jnp.where(c == column_of(r), 1.0, 0.0).astype(BF16)


def rms(x):
    return x * lax.rsqrt(jnp.mean(x * x, axis=-1, keepdims=True) + 1e-06)


def finish_pair(s, vst, ones, keys):
    s_lo, s_hi = s[:, :keys], s[:, keys:]
    p_lo = jnp.exp2(s_lo - jnp.max(s_lo, axis=-1, keepdims=True)).astype(BF16)
    p_hi = jnp.exp2(s_hi - jnp.max(s_hi, axis=-1, keepdims=True)).astype(BF16)
    p = jnp.concatenate([p_lo, p_hi], axis=1)
    o = dot(p, jnp.concatenate([vst, ones], axis=1))
    return (o[:, :128] / o[:, 128:]).astype(BF16)


def pipelined(blocks, scores, finish):
    ahead = scores(*blocks[0])
    for n, block in enumerate(blocks):
        now = ahead
        if n + 1 < len(blocks):
            ahead = scores(*blocks[n + 1])
        finish(now, *block)


def kernel(
    video, emb, cond, sgain, sqkv, sout, tgain, tqkv, tout, merge, cgain, cqkv, cout, up,
    out,
    vid, wcond, wsq, wso, wtq, wto, wm, wcq, wco, wup,
    sq, skst, svst, ones_s, smix,
    sbuf1, recv1,
    perm, spread, xt, tq, tkst, tvst, ones_t, tmix,
    sbuf2, cbuf, recv2,
    c0, cq, ck, cv, cmix, zs, zr,
    modv, lsem, vsem, osem, ss1, rs1, ss2, rs2, ss3, rs3,
):
    clip = lax.axis_index("clip")
    me = lax.axis_index("frame")
    z, x, y = me // 8, lax.rem(me // 2, 4), lax.rem(me, 2)

    def peer(o):
        return lax.rem(z + o[0], 4) * 8 + lax.rem(x + o[1], 4) * 2 + lax.rem(y + o[2], 2)

    barrier = pltpu.get_barrier_semaphore()
    for o in OFFSETS:
        pl.semaphore_signal(barrier, inc=1, device_id=(clip, peer(o)), device_id_type=MESH)

    weights = [
        (cond, wcond), (sqkv, wsq), (sout, wso), (tqkv, wtq), (tout, wto),
        (merge, wm), (cqkv, wcq), (cout, wco), (up, wup),
    ]
    wcopy = [pltpu.make_async_copy(a, b, lsem.at[i]) for i, (a, b) in enumerate(weights)]
    vcopy = [pltpu.make_async_copy(video.at[f], vid.at[f], vsem.at[f]) for f in range(4)]
    vcopy[0].start()
    for i in range(3):
        wcopy[i].start()
    for f in range(1, 4):
        vcopy[f].start()

    lane = lax.broadcasted_iota(jnp.int32, (1, 128), 1)
    lo = jnp.where(lane < HEAD, 1.0, 0.0).astype(F32)
    hi = 1.0 - lo
    ones_s[0:512, :] = jnp.broadcast_to(lo, (512, 128)).astype(BF16)
    ones_s[512:1024, :] = jnp.broadcast_to(hi, (512, 128)).astype(BF16)
    ones_t[0:128, :] = jnp.broadcast_to(lo, (128, 128)).astype(BF16)
    ones_t[128:256, :] = jnp.broadcast_to(hi, (128, 128)).astype(BF16)
    perm[0] = onehot(256, 256, lambda r: (r & 15) * 16 + (r >> 4))
    perm[1] = onehot(
        256, 256, lambda r: ((r >> 2) & 3) * 64 + ((r >> 4) & 3) * 16 + (r >> 6) * 4 + (r & 3)
    )
    for half in range(2):
        spread[half] = onehot(
            256, 64,
            lambda r: ((r >> 4) & 3) * 16 + half * 8 + (r >> 7) * 4 + ((r >> 2) & 3),
        )

    wcopy[0].wait()
    e1 = emb[...].astype(BF16).astype(F32)
    e2 = (emb[...] - e1).astype(BF16).astype(F32)
    e3 = emb[...] - e1 - e2
    piece = lax.broadcasted_iota(jnp.int32, (8, 128), 0)
    pieces = jnp.where(piece == 0, e1, jnp.where(piece == 1, e2, jnp.where(piece == 2, e3, 0.0)))
    modv[...] = jnp.sum(dot(pieces.astype(BF16), wcond[...]), axis=0, keepdims=True)
    sg = sgain[...] * (1.0 + modv[:, 0:D])
    shs = modv[:, D : 2 * D]
    tg = tgain[...] * (1.0 + modv[:, 2 * D : 3 * D])
    sht = modv[:, 3 * D : 4 * D]

    wcopy[1].wait()
    for i in range(3, 9):
        wcopy[i].start()
    pl.semaphore_wait(barrier, len(OFFSETS))

    def frame_step(f, carry):
        pltpu.make_async_copy(video.at[f], vid.at[f], vsem.at[f]).wait()
        xf = vid[f].astype(F32)
        normed = (rms(xf) * sg + shs).astype(BF16)
        sq[...] = (dot(normed, wsq[:, 0:D]) * QSCALE).astype(BF16)
        for p in range(4):
            k2 = dot(normed, wsq[:, D + p * 128 : D + (p + 1) * 128])
            skst[p, 0:512] = (k2 * lo).astype(BF16)
            skst[p, 512:1024] = (k2 * hi).astype(BF16)
            v2 = dot(normed, wsq[:, 2 * D + p * 128 : 2 * D + (p + 1) * 128])
            svst[p, 0:512] = (v2 * lo).astype(BF16)
            svst[p, 512:1024] = (v2 * hi).astype(BF16)

        def scores(p, i):
            return dot_t(sq[i * 256 : (i + 1) * 256, p * 128 : (p + 1) * 128], skst[p])

        def finish(v, p, i):
            smix[i * 256 : (i + 1) * 256, p * 128 : (p + 1) * 128] = finish_pair(
                v, svst[p], ones_s[...], 512
            )

        pipelined([(p, i) for p in range(4) for i in range(2)], scores, finish)

        @pl.when(f == 0)
        def _():
            wcopy[2].wait()

        sbuf1[f] = (vid[f].astype(F32) + dot(smix[...], wso[...])).astype(BF16)
        own = pl.ds(pl.multiple_of(me * 16, 16), 16)
        recv1[f * GROUP + me] = sbuf1[f, own, :]
        for o in OFFSETS:
            to = peer(o)
            pltpu.make_async_remote_copy(
                src_ref=sbuf1.at[f, pl.ds(pl.multiple_of(to * 16, 16), 16), :],
                dst_ref=recv1.at[f * GROUP + me],
                send_sem=ss1,
                recv_sem=rs1.at[f],
                device_id=(clip, to),
                device_id_type=MESH,
            ).start()
        return carry

    lax.fori_loop(0, 4, frame_step, 0)

    wcopy[3].wait()
    wcopy[4].wait()

    def group_step(j, carry):
        pltpu.make_async_copy(recv1.at[pl.ds(0, 31)], recv1.at[pl.ds(0, 31)], rs1.at[j]).wait()
        for sb in range(2):
            base = j * GROUP + sb * 16
            frames = pl.ds(pl.multiple_of(base, 16), 16)
            high = pl.ds(pl.multiple_of(128 + base, 16), 16)
            yg = dot(perm[0], recv1[frames].reshape(256, D))
            xt[:, frames, :] = yg.astype(BF16).reshape(16, 16, D)
            normed = (rms(yg) * tg + sht).astype(BF16)
            tq[:, frames, :] = (dot(normed, wtq[:, 0:D]) * QSCALE).astype(BF16).reshape(16, 16, D)
            for p in range(4):
                k2 = dot(normed, wtq[:, D + p * 128 : D + (p + 1) * 128])
                tkst[:, p, frames, :] = (k2 * lo).astype(BF16).reshape(16, 16, 128)
                tkst[:, p, high, :] = (k2 * hi).astype(BF16).reshape(16, 16, 128)
                v2 = dot(normed, wtq[:, 2 * D + p * 128 : 2 * D + (p + 1) * 128])
                tvst[:, p, frames, :] = (v2 * lo).astype(BF16).reshape(16, 16, 128)
                tvst[:, p, high, :] = (v2 * hi).astype(BF16).reshape(16, 16, 128)
        return carry

    lax.fori_loop(0, 4, group_step, 0)

    def token_step(c, carry):
        def scores(q, p):
            return dot_t(tq[c * 4 + q, :, p * 128 : (p + 1) * 128], tkst[c * 4 + q, p])

        def finish(v, q, p):
            tmix[q, :, p * 128 : (p + 1) * 128] = finish_pair(
                v, tvst[c * 4 + q, p], ones_t[...], 128
            )

        pipelined([(q, p) for q in range(4) for p in range(4)], scores, finish)
        for q in range(4):
            tmix[q] = (xt[c * 4 + q].astype(F32) + dot(tmix[q], wto[...])).astype(BF16)
        for sb in range(2):
            fg = jnp.concatenate(
                [
                    tmix[q, j * GROUP + sb * 16 : j * GROUP + (sb + 1) * 16, :]
                    for j in range(4) for q in range(4)
                ],
                axis=0,
            )
            sbuf2[c, sb * 16 : (sb + 1) * 16] = dot(perm[0], fg).astype(BF16).reshape(16, 16, D)
        recv2[c, me] = sbuf2[c, me]
        for o in OFFSETS:
            to = peer(o)
            pltpu.make_async_remote_copy(
                src_ref=sbuf2.at[c, to],
                dst_ref=recv2.at[c, me],
                send_sem=ss2,
                recv_sem=rs2,
                device_id=(clip, to),
                device_id_type=MESH,
            ).start()
        for d in range(2):
            for q in range(4):
                for jh in range(2):
                    j = 2 * jh + d
                    cbuf[
                        pl.ds(pl.multiple_of(c * 64 + jh * 32, 32), 32),
                        (d * 4 + q) * D : (d * 4 + q + 1) * D,
                    ] = tmix[q, j * GROUP : (j + 1) * GROUP, :]
        return carry

    lax.fori_loop(0, 4, token_step, 0)
    mine = pl.ds(pl.multiple_of(me * 16, 16), 16)

    for i in range(5, 9):
        wcopy[i].wait()
    c0[...] = dot(cbuf[...], wm[...]).astype(BF16)
    normed = (rms(c0[...].astype(F32)) * cgain[...]).astype(BF16)
    cq[...] = (dot(normed, wcq[:, 0:DC]) * QSCALE).astype(BF16)
    ck[...] = dot(normed, wcq[:, DC : 2 * DC]).astype(BF16)
    cv[...] = dot(normed, wcq[:, 2 * DC : 3 * DC]).astype(BF16)
    lane4 = lax.broadcasted_iota(jnp.int32, (64, 256), 1) >> 6
    block4 = jnp.concatenate(
        [jnp.where(lane4 == h, 1.0, 0.0).astype(BF16) for h in range(4)], axis=0
    )
    low = lax.broadcasted_iota(jnp.int32, (64, 128), 1) < HEAD

    def cell_scores(b, hg):
        rows, lanes = slice(b * 64, (b + 1) * 64), slice(hg * 256, (hg + 1) * 256)
        return dot_t(cq[rows, lanes], jnp.concatenate([ck[rows, lanes]] * 4, axis=0) * block4)

    def cell_finish(s, b, hg):
        rows, lanes = slice(b * 64, (b + 1) * 64), slice(hg * 256, (hg + 1) * 256)
        parts = []
        for half in range(2):
            sh = s[:, half * 128 : (half + 1) * 128]
            m_lo = jnp.max(jnp.where(low, sh, -jnp.inf), axis=-1, keepdims=True)
            m_hi = jnp.max(jnp.where(low, -jnp.inf, sh), axis=-1, keepdims=True)
            parts.append(jnp.exp2(sh - jnp.where(low, m_lo, m_hi)).astype(BF16))
        p = jnp.concatenate(parts, axis=1)
        o = dot(p, jnp.concatenate([cv[rows, lanes]] * 4, axis=0) * block4)
        cmix[rows, lanes] = (o / dot(p, block4)).astype(BF16)

    pipelined([(b, hg) for b in range(4) for hg in range(4)], cell_scores, cell_finish)
    coarse1 = (c0[...].astype(F32) + dot(cmix[...], wco[...])).astype(BF16)
    upped = dot(coarse1, wup[...]).astype(BF16)

    def pick(half):
        r = lax.broadcasted_iota(jnp.int32, (512, 256), 0)
        c = lax.broadcasted_iota(jnp.int32, (512, 256), 1)
        hit = (c == (r & 3) * 64 + ((r >> 2) & 1) * 32 + (r >> 4)) & (((r >> 3) & 1) == half)
        return jnp.where(hit, 1.0, 0.0).astype(BF16)

    zs[...] = (dot(pick(0), upped[:, :256]) + dot(pick(1), upped[:, 256:])).astype(BF16)
    zr[mine, :] = zs[mine, :]
    for o in OFFSETS:
        to = peer(o)
        pltpu.make_async_remote_copy(
            src_ref=zs.at[pl.ds(pl.multiple_of(to * 16, 16), 16), :],
            dst_ref=zr.at[mine, :],
            send_sem=ss3,
            recv_sem=rs3,
            device_id=(clip, to),
            device_id_type=MESH,
        ).start()

    pltpu.make_async_copy(recv2.at[:, pl.ds(0, 31)], recv2.at[:, pl.ds(0, 31)], rs2).wait()
    pltpu.make_async_copy(zr.at[pl.ds(0, 496)], zr.at[pl.ds(0, 496)], rs3).wait()
    ocopy = []
    for sb in range(8):
        got = jnp.concatenate(
            [recv2[c, sb * 4 : (sb + 1) * 4].reshape(64, D) for c in range(4)], axis=0
        )
        coarse = zr[sb * 64 : (sb + 1) * 64, :]
        for half in range(2):
            lanes = slice(half * 256, (half + 1) * 256)
            total = dot(perm[1], got[:, lanes]) + dot(spread[half], coarse)
            for j in range(4):
                vid[j, sb * 64 : (sb + 1) * 64, lanes] = total[j * 64 : (j + 1) * 64].astype(BF16)
        rows = pl.ds(sb * 64, 64)
        cp = pltpu.make_async_copy(vid.at[:, rows, :], out.at[:, rows, :], osem.at[sb])
        cp.start()
        ocopy.append(cp)
    pltpu.make_async_copy(sbuf1.at[:, pl.ds(0, 496), :], sbuf1.at[:, pl.ds(0, 496), :], ss1).wait()
    pltpu.make_async_copy(sbuf2.at[:, pl.ds(0, 31)], sbuf2.at[:, pl.ds(0, 31)], ss2).wait()
    pltpu.make_async_copy(zs.at[pl.ds(0, 496)], zs.at[pl.ds(0, 496)], ss3).wait()
    for cp in ocopy:
        cp.wait()


def body(
    video, timestep, cond_weight, spatial_gain, spatial_qkv, spatial_out, temporal_gain,
    temporal_qkv, temporal_out, merge_weight, coarse_gain, coarse_qkv, coarse_out, up_weight,
):
    counter = jnp.arange(FREQ, dtype=F32)
    frequency = jnp.exp(counter * (-math.log(10000.0) / FREQ))
    angles = timestep.astype(F32)[0] * frequency
    emb = jnp.concatenate([jnp.sin(angles), jnp.cos(angles)])[None]
    any_, vm = pl.BlockSpec(memory_space=pl.ANY), pl.BlockSpec(memory_space=pltpu.VMEM)
    b = lambda *shape: pltpu.VMEM(shape, BF16)
    return pl.pallas_call(
        kernel,
        name="denoise",
        out_shape=jax.ShapeDtypeStruct(video.shape, BF16),
        in_specs=[any_, vm, any_, vm, any_, any_, vm, any_, any_, any_, vm, any_, any_, any_],
        out_specs=any_,
        scratch_shapes=[
            b(4, 512, D), b(128, 2048), b(D, 3 * D), b(D, D), b(D, 3 * D), b(D, D),
            b(8 * D, DC), b(DC, 3 * DC), b(DC, DC), b(DC, D),
            b(512, D), b(4, 1024, 128), b(4, 1024, 128), b(1024, 128), b(512, D),
            b(4, 512, D), b(128, 16, D),
            b(2, 256, 256), b(2, 256, 64), b(16, 128, D), b(16, 128, D), b(16, 4, 256, 128),
            b(16, 4, 256, 128), b(256, 128), b(4, 128, D),
            b(4, 32, 16, D), b(256, 8 * D), b(4, 32, 16, D),
            b(256, DC), b(256, DC), b(256, DC), b(256, DC), b(256, DC), b(512, 256), b(512, 256),
            pltpu.VMEM((1, 4 * D), F32),
            pltpu.SemaphoreType.DMA((9,)), pltpu.SemaphoreType.DMA((4,)),
            pltpu.SemaphoreType.DMA((8,)),
            pltpu.SemaphoreType.DMA, pltpu.SemaphoreType.DMA((4,)),
        ] + [pltpu.SemaphoreType.DMA] * 4,
        compiler_params=pltpu.CompilerParams(
            collective_id=0, has_side_effects=True, vmem_limit_bytes=67_000_000
        ),
    )(
        video, emb, cond_weight, spatial_gain[None], spatial_qkv, spatial_out,
        temporal_gain[None], temporal_qkv, temporal_out, merge_weight, coarse_gain[None],
        coarse_qkv, coarse_out, up_weight,
    )


def solution(mesh):
    return jax.shard_map(
        body,
        mesh=mesh,
        in_specs=(P(("clip", "frame"), None, None), P("clip")) + (P(),) * 12,
        out_specs=P(("clip", "frame"), None, None),
        check_vma=False,
    )
```

time: 107 us -> 76.4 us (0.71)
  Pallas kernels: 102 us -> 70.9 us
    pallas_call x1, Pallas kernels: 102 us -> 70.9 us  [body(): pl.pallas_call(kernel, name='denoise', out_shape=jax.ShapeDtypeStruct(vid...]
where the time goes in v1:
time: 76.4 us; the launch traced here: 75.2 us
  Pallas kernels  70.9 us (93%)
  local copies, waits for them, and re-layouts  3.05 us (4%)
    pallas_call x1, Pallas kernels, body(): pl.pallas_call(kernel, name='denoise', out_shape=jax.ShapeDtypeStruct(vid...  70.9 us
    unnamed x1, local copies, waits for them, and re-layouts  3.05 us

profile of v1, /device:TPU:2, one launch (start us, length us, event | category | flops | bytes accessed | tf_op | source)
XLA Modules:
  0.0 75.2 jit_solution(3664029492946324297)
XLA Ops:
  0.7 0.6 maximum_bitcast_fusion.emb
  1.3 70.9 %denoise.1 = bf16[4,512,512]{2,1,0:T(8,128)(2,1)} custom-call(bf16[4,512,512]{2,1,0:T(8,128)(2,1)} %video.1, f32[1,128]{1,0:T(1,128)} %maximum_bitcast_fusion.emb, bf16[128,2048]{1,0:T(8,128)(2,1)} %cond.1, f32[1,512]{1,0:T(1,128)} %bitcast.7, bf16[512,1536]{1,0:T(8,128)(2,1)} %sqkv.1, bf16[512,512]{1,0:T(8,128)(2,1)} %sout.1, f32[1,512]{1,0:T(1,128)} %bitcast.8, ...), custom_call_target="tpu_custom_call" | custom-call | tf_op jit(solution)/shard_map/denoise/pallas_call | solution.py:329
  72.2 3.0 %copy.17 = bf16[4,512,512]{2,1,0:T(8,128)(2,1)} copy(bf16[4,512,512]{2,1,0:T(8,128)(2,1)} %denoise.1) | data formatting | bytes 4194304
  (1 shorter events, 0.0 us)

commit v2 on v1

--- a/solution.py
+++ b/solution.py
@@ -61,13 +61,13 @@
 
 def kernel(
     video, emb, cond, sgain, sqkv, sout, tgain, tqkv, tout, merge, cgain, cqkv, cout, up,
-    out,
+    recv2, zr,
     vid, wcond, wsq, wso, wtq, wto, wm, wcq, wco, wup,
     sq, skst, svst, ones_s, smix,
     sbuf1, recv1,
-    perm, spread, xt, tq, tkst, tvst, ones_t, tmix,
-    sbuf2, cbuf, recv2,
-    c0, cq, ck, cv, cmix, zs, zr,
+    perm, xt, tq, tkst, tvst, ones_t, tmix,
+    sbuf2, cbuf,
+    c0, cq, ck, cv, cmix, zs,
     modv, lsem, vsem, osem, ss1, rs1, ss2, rs2, ss3, rs3,
 ):
     clip = lax.axis_index("clip")
@@ -100,15 +100,7 @@
     ones_s[512:1024, :] = jnp.broadcast_to(hi, (512, 128)).astype(BF16)
     ones_t[0:128, :] = jnp.broadcast_to(lo, (128, 128)).astype(BF16)
     ones_t[128:256, :] = jnp.broadcast_to(hi, (128, 128)).astype(BF16)
-    perm[0] = onehot(256, 256, lambda r: (r & 15) * 16 + (r >> 4))
-    perm[1] = onehot(
-        256, 256, lambda r: ((r >> 2) & 3) * 64 + ((r >> 4) & 3) * 16 + (r >> 6) * 4 + (r & 3)
-    )
-    for half in range(2):
-        spread[half] = onehot(
-            256, 64,
-            lambda r: ((r >> 4) & 3) * 16 + half * 8 + (r >> 7) * 4 + ((r >> 2) & 3),
-        )
+    perm[...] = onehot(256, 256, lambda r: (r & 15) * 16 + (r >> 4))
 
     wcopy[0].wait()
     e1 = emb[...].astype(BF16).astype(F32)
@@ -123,9 +115,9 @@
     sht = modv[:, 3 * D : 4 * D]
 
     wcopy[1].wait()
+    wcopy[2].wait()
     for i in range(3, 9):
         wcopy[i].start()
-    pl.semaphore_wait(barrier, len(OFFSETS))
 
     def frame_step(f, carry):
         pltpu.make_async_copy(video.at[f], vid.at[f], vsem.at[f]).wait()
@@ -140,33 +132,38 @@
             svst[p, 0:512] = (v2 * lo).astype(BF16)
             svst[p, 512:1024] = (v2 * hi).astype(BF16)
 
-        def scores(p, i):
-            return dot_t(sq[i * 256 : (i + 1) * 256, p * 128 : (p + 1) * 128], skst[p])
-
-        def finish(v, p, i):
-            smix[i * 256 : (i + 1) * 256, p * 128 : (p + 1) * 128] = finish_pair(
-                v, svst[p], ones_s[...], 512
-            )
-
-        pipelined([(p, i) for p in range(4) for i in range(2)], scores, finish)
-
         @pl.when(f == 0)
         def _():
-            wcopy[2].wait()
-
-        sbuf1[f] = (vid[f].astype(F32) + dot(smix[...], wso[...])).astype(BF16)
-        own = pl.ds(pl.multiple_of(me * 16, 16), 16)
-        recv1[f * GROUP + me] = sbuf1[f, own, :]
-        for o in OFFSETS:
-            to = peer(o)
-            pltpu.make_async_remote_copy(
-                src_ref=sbuf1.at[f, pl.ds(pl.multiple_of(to * 16, 16), 16), :],
-                dst_ref=recv1.at[f * GROUP + me],
-                send_sem=ss1,
-                recv_sem=rs1.at[f],
-                device_id=(clip, to),
-                device_id_type=MESH,
-            ).start()
+            pl.semaphore_wait(barrier, len(OFFSETS))
+
+        def rows_of(dz):
+            return pl.ds(pl.multiple_of(lax.rem(z + dz, 4) * 128, 128), 128)
+
+        def scores(dz, p):
+            return dot_t(sq[rows_of(dz), p * 128 : (p + 1) * 128], skst[p])
+
+        def finish(v, dz, p):
+            rows = rows_of(dz)
+            smix[rows, p * 128 : (p + 1) * 128] = finish_pair(v, svst[p], ones_s[...], 512)
+            if p < 3:
+                return
+            sbuf1[f, rows, :] = (vid[f, rows, :].astype(F32) + dot(smix[rows, :], wso[...])).astype(BF16)
+            if dz == 0:
+                own = pl.ds(pl.multiple_of(me * 16, 16), 16)
+                recv1[f * GROUP + me] = sbuf1[f, own, :]
+            for o in OFFSETS:
+                if o[0] == dz:
+                    to = peer(o)
+                    pltpu.make_async_remote_copy(
+                        src_ref=sbuf1.at[f, pl.ds(pl.multiple_of(to * 16, 16), 16), :],
+                        dst_ref=recv1.at[f * GROUP + me],
+                        send_sem=ss1,
+                        recv_sem=rs1.at[f],
+                        device_id=(clip, to),
+                        device_id_type=MESH,
+                    ).start()
+
+        pipelined([(dz, p) for dz in (2, 1, 3, 0) for p in range(4)], scores, finish)
         return carry
 
     lax.fori_loop(0, 4, frame_step, 0)
@@ -180,7 +177,7 @@
             base = j * GROUP + sb * 16
             frames = pl.ds(pl.multiple_of(base, 16), 16)
             high = pl.ds(pl.multiple_of(128 + base, 16), 16)
-            yg = dot(perm[0], recv1[frames].reshape(256, D))
+            yg = dot(perm[...], recv1[frames].reshape(256, D))
             xt[:, frames, :] = yg.astype(BF16).reshape(16, 16, D)
             normed = (rms(yg) * tg + sht).astype(BF16)
             tq[:, frames, :] = (dot(normed, wtq[:, 0:D]) * QSCALE).astype(BF16).reshape(16, 16, D)
@@ -215,8 +212,8 @@
                 ],
                 axis=0,
             )
-            sbuf2[c, sb * 16 : (sb + 1) * 16] = dot(perm[0], fg).astype(BF16).reshape(16, 16, D)
-        recv2[c, me] = sbuf2[c, me]
+            sbuf2[c, sb * 16 : (sb + 1) * 16] = dot(perm[...], fg).astype(BF16).reshape(16, 16, D)
+        pltpu.make_async_copy(sbuf2.at[c, me], recv2.at[c, me], osem.at[c]).start()
         for o in OFFSETS:
             to = peer(o)
             pltpu.make_async_remote_copy(
@@ -280,7 +277,8 @@
         return jnp.where(hit, 1.0, 0.0).astype(BF16)
 
     zs[...] = (dot(pick(0), upped[:, :256]) + dot(pick(1), upped[:, 256:])).astype(BF16)
-    zr[mine, :] = zs[mine, :]
+    own_z = pltpu.make_async_copy(zs.at[mine], zr.at[mine], osem.at[4])
+    own_z.start()
     for o in OFFSETS:
         to = peer(o)
         pltpu.make_async_remote_copy(
@@ -294,24 +292,50 @@
 
     pltpu.make_async_copy(recv2.at[:, pl.ds(0, 31)], recv2.at[:, pl.ds(0, 31)], rs2).wait()
     pltpu.make_async_copy(zr.at[pl.ds(0, 496)], zr.at[pl.ds(0, 496)], rs3).wait()
-    ocopy = []
-    for sb in range(8):
-        got = jnp.concatenate(
-            [recv2[c, sb * 4 : (sb + 1) * 4].reshape(64, D) for c in range(4)], axis=0
-        )
-        coarse = zr[sb * 64 : (sb + 1) * 64, :]
-        for half in range(2):
-            lanes = slice(half * 256, (half + 1) * 256)
-            total = dot(perm[1], got[:, lanes]) + dot(spread[half], coarse)
-            for j in range(4):
-                vid[j, sb * 64 : (sb + 1) * 64, lanes] = total[j * 64 : (j + 1) * 64].astype(BF16)
-        rows = pl.ds(sb * 64, 64)
-        cp = pltpu.make_async_copy(vid.at[:, rows, :], out.at[:, rows, :], osem.at[sb])
-        cp.start()
-        ocopy.append(cp)
     pltpu.make_async_copy(sbuf1.at[:, pl.ds(0, 496), :], sbuf1.at[:, pl.ds(0, 496), :], ss1).wait()
     pltpu.make_async_copy(sbuf2.at[:, pl.ds(0, 31)], sbuf2.at[:, pl.ds(0, 31)], ss2).wait()
     pltpu.make_async_copy(zs.at[pl.ds(0, 496)], zs.at[pl.ds(0, 496)], ss3).wait()
+    for c in range(4):
+        pltpu.make_async_copy(sbuf2.at[c, me], recv2.at[c, me], osem.at[c]).wait()
+    own_z.wait()
+
+
+def combine(fine, coarse, out, got, zin, res, perm, spread, isem, osem):
+    def part(sb):
+        return pl.ds(sb * 4, 4)
+
+    zcopy = pltpu.make_async_copy(coarse, zin, isem.at[8])
+    zcopy.start()
+    icopy = [
+        pltpu.make_async_copy(fine.at[:, part(sb)], got.at[:, part(sb)], isem.at[sb])
+        for sb in range(8)
+    ]
+    for cp in icopy:
+        cp.start()
+    perm[...] = onehot(
+        256, 256, lambda r: ((r >> 2) & 3) * 64 + ((r >> 4) & 3) * 16 + (r >> 6) * 4 + (r & 3)
+    )
+    for half in range(2):
+        spread[half] = onehot(
+            256, 64,
+            lambda r: ((r >> 4) & 3) * 16 + half * 8 + (r >> 7) * 4 + ((r >> 2) & 3),
+        )
+    zcopy.wait()
+    ocopy = []
+    for sb in range(8):
+        icopy[sb].wait()
+        rows = slice(sb * 64, (sb + 1) * 64)
+        cells = jnp.concatenate([got[c, part(sb)].reshape(64, D) for c in range(4)], axis=0)
+        for half in range(2):
+            lanes = slice(half * 256, (half + 1) * 256)
+            total = dot(perm[...], cells[:, lanes]) + dot(spread[half], zin[rows, :])
+            for j in range(4):
+                res[j, rows, lanes] = total[j * 64 : (j + 1) * 64].astype(BF16)
+        cp = pltpu.make_async_copy(
+            res.at[:, pl.ds(sb * 64, 64), :], out.at[:, pl.ds(sb * 64, 64), :], osem.at[sb]
+        )
+        cp.start()
+        ocopy.append(cp)
     for cp in ocopy:
         cp.wait()
 
@@ -326,21 +350,24 @@
     emb = jnp.concatenate([jnp.sin(angles), jnp.cos(angles)])[None]
     any_, vm = pl.BlockSpec(memory_space=pl.ANY), pl.BlockSpec(memory_space=pltpu.VMEM)
     b = lambda *shape: pltpu.VMEM(shape, BF16)
-    return pl.pallas_call(
+    fine, coarse = pl.pallas_call(
         kernel,
         name="denoise",
-        out_shape=jax.ShapeDtypeStruct(video.shape, BF16),
+        out_shape=[
+            jax.ShapeDtypeStruct((4, GROUP, 16, D), BF16),
+            jax.ShapeDtypeStruct((512, 256), BF16),
+        ],
         in_specs=[any_, vm, any_, vm, any_, any_, vm, any_, any_, any_, vm, any_, any_, any_],
-        out_specs=any_,
+        out_specs=[any_, any_],
         scratch_shapes=[
             b(4, 512, D), b(128, 2048), b(D, 3 * D), b(D, D), b(D, 3 * D), b(D, D),
             b(8 * D, DC), b(DC, 3 * DC), b(DC, DC), b(DC, D),
             b(512, D), b(4, 1024, 128), b(4, 1024, 128), b(1024, 128), b(512, D),
             b(4, 512, D), b(128, 16, D),
-            b(2, 256, 256), b(2, 256, 64), b(16, 128, D), b(16, 128, D), b(16, 4, 256, 128),
+            b(256, 256), b(16, 128, D), b(16, 128, D), b(16, 4, 256, 128),
             b(16, 4, 256, 128), b(256, 128), b(4, 128, D),
-            b(4, 32, 16, D), b(256, 8 * D), b(4, 32, 16, D),
-            b(256, DC), b(256, DC), b(256, DC), b(256, DC), b(256, DC), b(512, 256), b(512, 256),
+            b(4, 32, 16, D), b(256, 8 * D),
+            b(256, DC), b(256, DC), b(256, DC), b(256, DC), b(256, DC), b(512, 256),
             pltpu.VMEM((1, 4 * D), F32),
             pltpu.SemaphoreType.DMA((9,)), pltpu.SemaphoreType.DMA((4,)),
             pltpu.SemaphoreType.DMA((8,)),
@@ -354,6 +381,17 @@
         temporal_gain[None], temporal_qkv, temporal_out, merge_weight, coarse_gain[None],
         coarse_qkv, coarse_out, up_weight,
     )
+    return pl.pallas_call(
+        combine,
+        name="combine",
+        out_shape=jax.ShapeDtypeStruct(video.shape, BF16),
+        in_specs=[any_, any_],
+        out_specs=any_,
+        scratch_shapes=[
+            b(4, GROUP, 16, D), b(512, 256), b(4, 512, D), b(256, 256), b(2, 256, 64),
+            pltpu.SemaphoreType.DMA((9,)), pltpu.SemaphoreType.DMA((8,)),
+        ],
+    )(fine, coarse)
 
 
 def solution(mesh):

time: 76.4 us -> 74.9 us (0.980)
  local copies, waits for them, and re-layouts: 3.05 us -> 0 us
  Pallas kernels: 70.9 us -> 72.1 us
    unnamed x1 -> x0, local copies, waits for them, and re-layouts: 3.05 us -> none
    pallas_call x1 -> x2, Pallas kernels: 70.9 us -> 72.1 us  [the longest x1 68 us: body(): pl.pallas_call(kernel, name='denoise', out_shape=[jax.ShapeDtypeStruct((4...]
where the time goes in v2:
time: 74.9 us; the launch traced here: 73.5 us
  Pallas kernels  72.1 us (96%)
  between operations  0.83 us (1%)
    pallas_call x1, Pallas kernels, body(): pl.pallas_call(kernel, name='denoise', out_shape=[jax.ShapeDtypeStruct((4...  68 us
    pallas_call x1, Pallas kernels, body(): pl.pallas_call(combine, name='combine', out_shape=jax.ShapeDtypeStruct(vi...  4.1 us

profile of v2, /device:TPU:2, one launch (start us, length us, event | category | flops | bytes accessed | tf_op | source)
XLA Modules:
  0.0 73.5 jit_solution(6747494261083403666)
XLA Ops:
  0.7 0.6 maximum_bitcast_fusion.emb
  1.3 68.0 %denoise.1 = (bf16[4,32,16,512]{3,2,1,0:T(8,128)(2,1)}, bf16[512,256]{1,0:T(8,128)(2,1)}) custom-call(bf16[4,512,512]{2,1,0:T(8,128)(2,1)} %video.1, f32[1,128]{1,0:T(1,128)} %maximum_bitcast_fusion.emb, bf16[128,2048]{1,0:T(8,128)(2,1)} %cond.1, f32[1,512]{1,0:T(1,128)} %bitcast.7, bf16[512,1536]{1,0:T(8,128)(2,1)} %sqkv.1, bf16[512,512]{1,0:T(8,128)(2,1)} %sout.1, ...), custom_call_target="tpu_custom_call" | custom-call | tf_op jit(solution)/shard_map/denoise/pallas_call | solution.py:353
  69.3 4.1 %combine.1 = bf16[4,512,512]{2,1,0:T(8,128)(2,1)} custom-call(bf16[4,32,16,512]{3,2,1,0:T(8,128)(2,1)} %get-tuple-element.7.fine, bf16[512,256]{1,0:T(8,128)(2,1)} %get-tuple-element.8.coarse), custom_call_target="tpu_custom_call" | custom-call | tf_op jit(solution)/shard_map/combine/pallas_call | solution.py:384
  (1 shorter events, 0.0 us)

commit v3 on v2

--- a/solution.py
+++ b/solution.py
@@ -31,10 +31,13 @@
     return lax.dot_general(a, b, (((1,), (1,)), ((), ())), preferred_element_type=F32)
 
 
-def onehot(rows, columns, column_of):
+def onehot(rows, columns, column_of, keep=None):
     r = lax.broadcasted_iota(jnp.int32, (rows, columns), 0)
     c = lax.broadcasted_iota(jnp.int32, (rows, columns), 1)
-    return jnp.where(c == column_of(r), 1.0, 0.0).astype(BF16)
+    hit = c == column_of(r)
+    if keep is not None:
+        hit = hit & keep(r)
+    return jnp.where(hit, 1.0, 0.0).astype(BF16)
 
 
 def rms(x):
@@ -64,11 +67,11 @@
     recv2, zr,
     vid, wcond, wsq, wso, wtq, wto, wm, wcq, wco, wup,
     sq, skst, svst, ones_s, smix,
-    sbuf1, recv1,
+    sbuf1, recv1, sbufl, recvl, esend, frecv,
     perm, xt, tq, tkst, tvst, ones_t, tmix,
     sbuf2, cbuf,
     c0, cq, ck, cv, cmix, zs,
-    modv, lsem, vsem, osem, ss1, rs1, ss2, rs2, ss3, rs3,
+    modv, lsem, vsem, osem, ss1, rs1, ss2, rs2, ss3, rs3, ssl, rsl,
 ):
     clip = lax.axis_index("clip")
     me = lax.axis_index("frame")
@@ -101,6 +104,13 @@
     ones_t[0:128, :] = jnp.broadcast_to(lo, (128, 128)).astype(BF16)
     ones_t[128:256, :] = jnp.broadcast_to(hi, (128, 128)).astype(BF16)
     perm[...] = onehot(256, 256, lambda r: (r & 15) * 16 + (r >> 4))
+    for h in range(2):
+        esend[h] = onehot(
+            256, 128,
+            lambda r: ((r >> 4) & 7) * 16 + (r >> 7) * 8 + (r & 7),
+            lambda r: ((r >> 3) & 1) == h,
+        )
+        frecv[h] = onehot(128, 256, lambda r: (r & 15) * 16 + h * 8 + (r >> 4))
 
     wcopy[0].wait()
     e1 = emb[...].astype(BF16).astype(F32)
@@ -119,7 +129,18 @@
     for i in range(3, 9):
         wcopy[i].start()
 
-    def frame_step(f, carry):
+    def send_late(half, o):
+        to = peer(o)
+        pltpu.make_async_remote_copy(
+            src_ref=sbufl.at[half, to],
+            dst_ref=recvl.at[half, me],
+            send_sem=ssl,
+            recv_sem=rsl.at[half],
+            device_id=(clip, to),
+            device_id_type=MESH,
+        ).start()
+
+    def frame_step(f, last):
         pltpu.make_async_copy(video.at[f], vid.at[f], vsem.at[f]).wait()
         xf = vid[f].astype(F32)
         normed = (rms(xf) * sg + shs).astype(BF16)
@@ -132,9 +153,11 @@
             svst[p, 0:512] = (v2 * lo).astype(BF16)
             svst[p, 512:1024] = (v2 * hi).astype(BF16)
 
-        @pl.when(f == 0)
-        def _():
-            pl.semaphore_wait(barrier, len(OFFSETS))
+        if not last:
+
+            @pl.when(f == 0)
+            def _():
+                pl.semaphore_wait(barrier, len(OFFSETS))
 
         def rows_of(dz):
             return pl.ds(pl.multiple_of(lax.rem(z + dz, 4) * 128, 128), 128)
@@ -147,7 +170,21 @@
             smix[rows, p * 128 : (p + 1) * 128] = finish_pair(v, svst[p], ones_s[...], 512)
             if p < 3:
                 return
-            sbuf1[f, rows, :] = (vid[f, rows, :].astype(F32) + dot(smix[rows, :], wso[...])).astype(BF16)
+            fine1 = (vid[f, rows, :].astype(F32) + dot(smix[rows, :], wso[...])).astype(BF16)
+            if last:
+                halves = dot(esend[0], fine1[:, :256]) + dot(esend[1], fine1[:, 256:])
+                halves = halves.astype(BF16).reshape(2, 8, 16, 256)
+                devices = pl.ds(lax.rem(z + dz, 4) * 8, 8)
+                sbufl[0, devices] = halves[0]
+                sbufl[1, devices] = halves[1]
+                if dz == 0:
+                    recvl[0, me] = sbufl[0, me]
+                    recvl[1, me] = sbufl[1, me]
+                for o in OFFSETS:
+                    if o[0] == dz:
+                        send_late(0, o)
+                return
+            sbuf1[f, rows, :] = fine1
             if dz == 0:
                 own = pl.ds(pl.multiple_of(me * 16, 16), 16)
                 recv1[f * GROUP + me] = sbuf1[f, own, :]
@@ -164,35 +201,61 @@
                     ).start()
 
         pipelined([(dz, p) for dz in (2, 1, 3, 0) for p in range(4)], scores, finish)
+        if last:
+            for o in OFFSETS:
+                send_late(1, o)
+
+    def early_frame(f, carry):
+        frame_step(f, False)
         return carry
 
-    lax.fori_loop(0, 4, frame_step, 0)
+    lax.fori_loop(0, 3, early_frame, 0)
+    frame_step(3, True)
 
     wcopy[3].wait()
     wcopy[4].wait()
+
+    def project(yg, tokens, base):
+        count = yg.shape[0] // 16
+        frames = pl.ds(pl.multiple_of(base, 16), 16)
+        high = pl.ds(pl.multiple_of(128 + base, 16), 16)
+        xt[tokens, frames, :] = yg.astype(BF16).reshape(count, 16, D)
+        normed = (rms(yg) * tg + sht).astype(BF16)
+        q = dot(normed, wtq[:, 0:D]) * QSCALE
+        tq[tokens, frames, :] = q.astype(BF16).reshape(count, 16, D)
+        for p in range(4):
+            k2 = dot(normed, wtq[:, D + p * 128 : D + (p + 1) * 128])
+            tkst[tokens, p, frames, :] = (k2 * lo).astype(BF16).reshape(count, 16, 128)
+            tkst[tokens, p, high, :] = (k2 * hi).astype(BF16).reshape(count, 16, 128)
+            v2 = dot(normed, wtq[:, 2 * D + p * 128 : 2 * D + (p + 1) * 128])
+            tvst[tokens, p, frames, :] = (v2 * lo).astype(BF16).reshape(count, 16, 128)
+            tvst[tokens, p, high, :] = (v2 * hi).astype(BF16).reshape(count, 16, 128)
 
     def group_step(j, carry):
         pltpu.make_async_copy(recv1.at[pl.ds(0, 31)], recv1.at[pl.ds(0, 31)], rs1.at[j]).wait()
         for sb in range(2):
             base = j * GROUP + sb * 16
             frames = pl.ds(pl.multiple_of(base, 16), 16)
-            high = pl.ds(pl.multiple_of(128 + base, 16), 16)
-            yg = dot(perm[...], recv1[frames].reshape(256, D))
-            xt[:, frames, :] = yg.astype(BF16).reshape(16, 16, D)
-            normed = (rms(yg) * tg + sht).astype(BF16)
-            tq[:, frames, :] = (dot(normed, wtq[:, 0:D]) * QSCALE).astype(BF16).reshape(16, 16, D)
-            for p in range(4):
-                k2 = dot(normed, wtq[:, D + p * 128 : D + (p + 1) * 128])
-                tkst[:, p, frames, :] = (k2 * lo).astype(BF16).reshape(16, 16, 128)
-                tkst[:, p, high, :] = (k2 * hi).astype(BF16).reshape(16, 16, 128)
-                v2 = dot(normed, wtq[:, 2 * D + p * 128 : 2 * D + (p + 1) * 128])
-                tvst[:, p, frames, :] = (v2 * lo).astype(BF16).reshape(16, 16, 128)
-                tvst[:, p, high, :] = (v2 * hi).astype(BF16).reshape(16, 16, 128)
+            project(dot(perm[...], recv1[frames].reshape(256, D)), slice(0, 16), base)
         return carry
 
-    lax.fori_loop(0, 4, group_step, 0)
+    def late_group(half):
+        pltpu.make_async_copy(
+            recvl.at[half, pl.ds(0, 31)], recvl.at[half, pl.ds(0, 31)], rsl.at[half]
+        ).wait()
+        for sb in range(2):
+            got = recvl[half, sb * 16 : (sb + 1) * 16].reshape(256, 256)
+            yg = jnp.concatenate([dot(frecv[0], got), dot(frecv[1], got)], axis=1)
+            project(yg, slice(half * 8, half * 8 + 8), 3 * GROUP + sb * 16)
+
+    lax.fori_loop(0, 3, group_step, 0)
+    late_group(0)
 
     def token_step(c, carry):
+        @pl.when(c == 2)
+        def _():
+            late_group(1)
+
         def scores(q, p):
             return dot_t(tq[c * 4 + q, :, p * 128 : (p + 1) * 128], tkst[c * 4 + q, p])
 
@@ -293,6 +356,7 @@
     pltpu.make_async_copy(recv2.at[:, pl.ds(0, 31)], recv2.at[:, pl.ds(0, 31)], rs2).wait()
     pltpu.make_async_copy(zr.at[pl.ds(0, 496)], zr.at[pl.ds(0, 496)], rs3).wait()
     pltpu.make_async_copy(sbuf1.at[:, pl.ds(0, 496), :], sbuf1.at[:, pl.ds(0, 496), :], ss1).wait()
+    pltpu.make_async_copy(sbufl.at[:, pl.ds(0, 31)], sbufl.at[:, pl.ds(0, 31)], ssl).wait()
     pltpu.make_async_copy(sbuf2.at[:, pl.ds(0, 31)], sbuf2.at[:, pl.ds(0, 31)], ss2).wait()
     pltpu.make_async_copy(zs.at[pl.ds(0, 496)], zs.at[pl.ds(0, 496)], ss3).wait()
     for c in range(4):
@@ -363,7 +427,8 @@
             b(4, 512, D), b(128, 2048), b(D, 3 * D), b(D, D), b(D, 3 * D), b(D, D),
             b(8 * D, DC), b(DC, 3 * DC), b(DC, DC), b(DC, D),
             b(512, D), b(4, 1024, 128), b(4, 1024, 128), b(1024, 128), b(512, D),
-            b(4, 512, D), b(128, 16, D),
+            b(3, 512, D), b(96, 16, D), b(2, GROUP, 16, 256), b(2, GROUP, 16, 256),
+            b(2, 256, 128), b(2, 128, 256),
             b(256, 256), b(16, 128, D), b(16, 128, D), b(16, 4, 256, 128),
             b(16, 4, 256, 128), b(256, 128), b(4, 128, D),
             b(4, 32, 16, D), b(256, 8 * D),
@@ -371,8 +436,8 @@
             pltpu.VMEM((1, 4 * D), F32),
             pltpu.SemaphoreType.DMA((9,)), pltpu.SemaphoreType.DMA((4,)),
             pltpu.SemaphoreType.DMA((8,)),
-            pltpu.SemaphoreType.DMA, pltpu.SemaphoreType.DMA((4,)),
-        ] + [pltpu.SemaphoreType.DMA] * 4,
+            pltpu.SemaphoreType.DMA, pltpu.SemaphoreType.DMA((3,)),
+        ] + [pltpu.SemaphoreType.DMA] * 5 + [pltpu.SemaphoreType.DMA((2,))],
         compiler_params=pltpu.CompilerParams(
             collective_id=0, has_side_effects=True, vmem_limit_bytes=67_000_000
         ),

time: 74.9 us -> 75.7 us (1.011)
  Pallas kernels: 72.1 us -> 72.9 us
    pallas_call x1, Pallas kernels: 68 us -> 68.7 us  [body(): pl.pallas_call(kernel, name='denoise', out_shape=[jax.ShapeDtypeStruct((4...]
where the time goes in v3:
time: 75.7 us; the launch traced here: 74.3 us
  Pallas kernels  72.9 us (96%)
  between operations  0.83 us (1%)
    pallas_call x1, Pallas kernels, body(): pl.pallas_call(kernel, name='denoise', out_shape=[jax.ShapeDtypeStruct((4...  68.7 us
    pallas_call x1, Pallas kernels, body(): pl.pallas_call(combine, name='combine', out_shape=jax.ShapeDtypeStruct(vi...  4.11 us

profile of v3, /device:TPU:2, one launch (start us, length us, event | category | flops | bytes accessed | tf_op | source)
XLA Modules:
  0.0 74.3 jit_solution(16961494313392063433)
XLA Ops:
  0.7 0.6 maximum_bitcast_fusion.emb
  1.3 68.7 %denoise.1 = (bf16[4,32,16,512]{3,2,1,0:T(8,128)(2,1)}, bf16[512,256]{1,0:T(8,128)(2,1)}) custom-call(bf16[4,512,512]{2,1,0:T(8,128)(2,1)} %video.1, f32[1,128]{1,0:T(1,128)} %maximum_bitcast_fusion.emb, bf16[128,2048]{1,0:T(8,128)(2,1)} %cond.1, f32[1,512]{1,0:T(1,128)} %bitcast.7, bf16[512,1536]{1,0:T(8,128)(2,1)} %sqkv.1, bf16[512,512]{1,0:T(8,128)(2,1)} %sout.1, ...), custom_call_target="tpu_custom_call" | custom-call | tf_op jit(solution)/shard_map/denoise/pallas_call | solution.py:417
  70.1 4.1 %combine.1 = bf16[4,512,512]{2,1,0:T(8,128)(2,1)} custom-call(bf16[4,32,16,512]{3,2,1,0:T(8,128)(2,1)} %get-tuple-element.7.fine, bf16[512,256]{1,0:T(8,128)(2,1)} %get-tuple-element.8.coarse), custom_call_target="tpu_custom_call" | custom-call | tf_op jit(solution)/shard_map/combine/pallas_call | solution.py:449
  (1 shorter events, 0.0 us)

commit v4 on v3

--- a/solution.py
+++ b/solution.py
@@ -201,9 +201,6 @@
                     ).start()
 
         pipelined([(dz, p) for dz in (2, 1, 3, 0) for p in range(4)], scores, finish)
-        if last:
-            for o in OFFSETS:
-                send_late(1, o)
 
     def early_frame(f, carry):
         frame_step(f, False)
@@ -233,6 +230,12 @@
 
     def group_step(j, carry):
         pltpu.make_async_copy(recv1.at[pl.ds(0, 31)], recv1.at[pl.ds(0, 31)], rs1.at[j]).wait()
+
+        @pl.when(j == 2)
+        def _():
+            for o in OFFSETS:
+                send_late(1, o)
+
         for sb in range(2):
             base = j * GROUP + sb * 16
             frames = pl.ds(pl.multiple_of(base, 16), 16)

time: 75.7 us -> 75.7 us (level)
  no operation moved by 1% of the time
where the time goes in v4:
time: 75.7 us; the launch traced here: 74.3 us
  Pallas kernels  72.9 us (96%)
  between operations  0.83 us (1%)
    pallas_call x1, Pallas kernels, body(): pl.pallas_call(kernel, name='denoise', out_shape=[jax.ShapeDtypeStruct((4...  68.7 us
    pallas_call x1, Pallas kernels, body(): pl.pallas_call(combine, name='combine', out_shape=jax.ShapeDtypeStruct(vi...  4.11 us

profile of v4, /device:TPU:2, one launch (start us, length us, event | category | flops | bytes accessed | tf_op | source)
XLA Modules:
  0.0 74.3 jit_solution(384426439389293993)
XLA Ops:
  0.7 0.6 maximum_bitcast_fusion.emb
  1.3 68.7 %denoise.1 = (bf16[4,32,16,512]{3,2,1,0:T(8,128)(2,1)}, bf16[512,256]{1,0:T(8,128)(2,1)}) custom-call(bf16[4,512,512]{2,1,0:T(8,128)(2,1)} %video.1, f32[1,128]{1,0:T(1,128)} %maximum_bitcast_fusion.emb, bf16[128,2048]{1,0:T(8,128)(2,1)} %cond.1, f32[1,512]{1,0:T(1,128)} %bitcast.7, bf16[512,1536]{1,0:T(8,128)(2,1)} %sqkv.1, bf16[512,512]{1,0:T(8,128)(2,1)} %sout.1, ...), custom_call_target="tpu_custom_call" | custom-call | tf_op jit(solution)/shard_map/denoise/pallas_call | solution.py:420
  70.1 4.1 %combine.1 = bf16[4,512,512]{2,1,0:T(8,128)(2,1)} custom-call(bf16[4,32,16,512]{3,2,1,0:T(8,128)(2,1)} %get-tuple-element.7.fine, bf16[512,256]{1,0:T(8,128)(2,1)} %get-tuple-element.8.coarse), custom_call_target="tpu_custom_call" | custom-call | tf_op jit(solution)/shard_map/combine/pallas_call | solution.py:452
  (1 shorter events, 0.0 us)

commit v5 on v2

--- a/solution.py
+++ b/solution.py
@@ -65,7 +65,7 @@
     vid, wcond, wsq, wso, wtq, wto, wm, wcq, wco, wup,
     sq, skst, svst, ones_s, smix,
     sbuf1, recv1,
-    perm, xt, tq, tkst, tvst, ones_t, tmix,
+    perm, xt, tn, tq, tkst, tvst, ones_t, tmix,
     sbuf2, cbuf,
     c0, cq, ck, cv, cmix, zs,
     modv, lsem, vsem, osem, ss1, rs1, ss2, rs2, ss3, rs3,
@@ -176,29 +176,30 @@
         for sb in range(2):
             base = j * GROUP + sb * 16
             frames = pl.ds(pl.multiple_of(base, 16), 16)
-            high = pl.ds(pl.multiple_of(128 + base, 16), 16)
             yg = dot(perm[...], recv1[frames].reshape(256, D))
             xt[:, frames, :] = yg.astype(BF16).reshape(16, 16, D)
-            normed = (rms(yg) * tg + sht).astype(BF16)
-            tq[:, frames, :] = (dot(normed, wtq[:, 0:D]) * QSCALE).astype(BF16).reshape(16, 16, D)
-            for p in range(4):
-                k2 = dot(normed, wtq[:, D + p * 128 : D + (p + 1) * 128])
-                tkst[:, p, frames, :] = (k2 * lo).astype(BF16).reshape(16, 16, 128)
-                tkst[:, p, high, :] = (k2 * hi).astype(BF16).reshape(16, 16, 128)
-                v2 = dot(normed, wtq[:, 2 * D + p * 128 : 2 * D + (p + 1) * 128])
-                tvst[:, p, frames, :] = (v2 * lo).astype(BF16).reshape(16, 16, 128)
-                tvst[:, p, high, :] = (v2 * hi).astype(BF16).reshape(16, 16, 128)
+            tn[:, frames, :] = (rms(yg) * tg + sht).astype(BF16).reshape(16, 16, D)
         return carry
 
     lax.fori_loop(0, 4, group_step, 0)
 
     def token_step(c, carry):
+        normed = tn[pl.ds(c * 4, 4)].reshape(512, D)
+        tq[...] = (dot(normed, wtq[:, 0:D]) * QSCALE).astype(BF16).reshape(4, 128, D)
+        for p in range(4):
+            k2 = dot(normed, wtq[:, D + p * 128 : D + (p + 1) * 128])
+            tkst[:, p, 0:128, :] = (k2 * lo).astype(BF16).reshape(4, 128, 128)
+            tkst[:, p, 128:256, :] = (k2 * hi).astype(BF16).reshape(4, 128, 128)
+            v2 = dot(normed, wtq[:, 2 * D + p * 128 : 2 * D + (p + 1) * 128])
+            tvst[:, p, 0:128, :] = (v2 * lo).astype(BF16).reshape(4, 128, 128)
+            tvst[:, p, 128:256, :] = (v2 * hi).astype(BF16).reshape(4, 128, 128)
+
         def scores(q, p):
-            return dot_t(tq[c * 4 + q, :, p * 128 : (p + 1) * 128], tkst[c * 4 + q, p])
+            return dot_t(tq[q, :, p * 128 : (p + 1) * 128], tkst[q, p])
 
         def finish(v, q, p):
             tmix[q, :, p * 128 : (p + 1) * 128] = finish_pair(
-                v, tvst[c * 4 + q, p], ones_t[...], 128
+                v, tvst[q, p], ones_t[...], 128
             )
 
         pipelined([(q, p) for q in range(4) for p in range(4)], scores, finish)
@@ -364,8 +365,8 @@
             b(8 * D, DC), b(DC, 3 * DC), b(DC, DC), b(DC, D),
             b(512, D), b(4, 1024, 128), b(4, 1024, 128), b(1024, 128), b(512, D),
             b(4, 512, D), b(128, 16, D),
-            b(256, 256), b(16, 128, D), b(16, 128, D), b(16, 4, 256, 128),
-            b(16, 4, 256, 128), b(256, 128), b(4, 128, D),
+            b(256, 256), b(16, 128, D), b(16, 128, D), b(4, 128, D), b(4, 4, 256, 128),
+            b(4, 4, 256, 128), b(256, 128), b(4, 128, D),
             b(4, 32, 16, D), b(256, 8 * D),
             b(256, DC), b(256, DC), b(256, DC), b(256, DC), b(256, DC), b(512, 256),
             pltpu.VMEM((1, 4 * D), F32),

time: 74.9 us -> 73.5 us (0.981)
  Pallas kernels: 72.1 us -> 71.2 us
    pallas_call x1, Pallas kernels: 68 us -> 67.1 us  [body(): pl.pallas_call(kernel, name='denoise', out_shape=[jax.ShapeDtypeStruct((4...]
where the time goes in v5:
time: 73.5 us; the launch traced here: 72.7 us
  Pallas kernels  71.2 us (97%)
  between operations  0.83 us (1%)
    pallas_call x1, Pallas kernels, body(): pl.pallas_call(kernel, name='denoise', out_shape=[jax.ShapeDtypeStruct((4...  67.1 us
    pallas_call x1, Pallas kernels, body(): pl.pallas_call(combine, name='combine', out_shape=jax.ShapeDtypeStruct(vi...  4.11 us

profile of v5, /device:TPU:2, one launch (start us, length us, event | category | flops | bytes accessed | tf_op | source)
XLA Modules:
  0.0 72.7 jit_solution(9725281153974773928)
XLA Ops:
  0.7 0.6 maximum_bitcast_fusion.emb
  1.3 67.1 %denoise.1 = (bf16[4,32,16,512]{3,2,1,0:T(8,128)(2,1)}, bf16[512,256]{1,0:T(8,128)(2,1)}) custom-call(bf16[4,512,512]{2,1,0:T(8,128)(2,1)} %video.1, f32[1,128]{1,0:T(1,128)} %maximum_bitcast_fusion.emb, bf16[128,2048]{1,0:T(8,128)(2,1)} %cond.1, f32[1,512]{1,0:T(1,128)} %bitcast.7, bf16[512,1536]{1,0:T(8,128)(2,1)} %sqkv.1, bf16[512,512]{1,0:T(8,128)(2,1)} %sout.1, ...), custom_call_target="tpu_custom_call" | custom-call | tf_op jit(solution)/shard_map/denoise/pallas_call | solution.py:354
  68.4 4.1 %combine.1 = bf16[4,512,512]{2,1,0:T(8,128)(2,1)} custom-call(bf16[4,32,16,512]{3,2,1,0:T(8,128)(2,1)} %get-tuple-element.7.fine, bf16[512,256]{1,0:T(8,128)(2,1)} %get-tuple-element.8.coarse), custom_call_target="tpu_custom_call" | custom-call | tf_op jit(solution)/shard_map/combine/pallas_call | solution.py:385
  (1 shorter events, 0.0 us)
